TPU v7x, 128 devices: a whole 4x4x4 slice. The times are simulated.
128 devices in a mesh: dp: 16 (over y, x_hi, core), fsdp: 8 (over z, x_lo).
Axes of the slice: x: 4 (x_hi: 2, x_lo: 2; x = x_hi * 2 + x_lo), y: 4, z: 4, core: 2. Of those that a mesh axis runs over, the one named last changes fastest.
Arguments:
- acts: bfloat16 [65536, 8192], P(('dp', 'fsdp')), may hold values from -24 to 24
- grad_out: bfloat16 [65536, 1024], P(('dp', 'fsdp')), may hold values from -24 to 24
- codes: int32 [128, 16, 1024], P('fsdp'), may hold values from 0 to 65535
- scale_codes: int32 [128, 1024], P('fsdp'), may hold values from 0 to 255
- col_scale: float32 [1024], replicated, may hold values from 0.03 to 0.3
- down_adapter: bfloat16 [64, 8192], P(None, 'fsdp'), may hold values from -0.1796875 to 0.1796875
- up_adapter: bfloat16 [64, 1024], P(None, 'fsdp'), may hold values from -0.1875 to 0.1875
Outputs:
- input_gradient: bfloat16 [65536, 8192], P(('dp', 'fsdp'))
- grad_down: float32 [64, 8192], P(None, 'fsdp')
- grad_up: float32 [64, 1024], P(None, 'fsdp')
All inputs are finite; a program needn't handle non-finite values.
Results may differ from a plain program's by a relative error of at most 0.0059.
Values may be sent and summed in bfloat16 or wider, within the bound.
No kernel may reach another device: no remote copies, remote signals or barrier semaphores. Data moves between devices by JAX's collectives and lax.ppermute only.
A program may use at most 128 MiB of HBM per device.

v0:
```python
import jax
import jax.numpy as jnp
from jax import lax
from jax.sharding import PartitionSpec as P

adapter_scale = 0.5
nf4_table = [
    -1.0,
    -0.6961928009986877,
    -0.5250730514526367,
    -0.39491748809814453,
    -0.28444138169288635,
    -0.18477343022823334,
    -0.09105003625154495,
    0.0,
    0.07958029955625534,
    0.16093020141124725,
    0.24611230194568634,
    0.33791524171829224,
    0.44070982933044434,
    0.5626170039176941,
    0.7229568362236023,
    1.0,
]


def joined_along(tiles, dim):
    tiles = jnp.moveaxis(tiles, 0, dim)
    lengths = tiles.shape
    return tiles.reshape(*lengths[:dim], lengths[dim] * lengths[dim + 1], *lengths[dim + 2 :])


def gather_packed(arrays, axis, dims):
    flat = jnp.concatenate([a.reshape(-1) for a in arrays])
    lines, at, gathered = (lax.all_gather(flat, axis), 0, [])
    for a, dim in zip(arrays, dims):
        tiles = lines[:, at : at + a.size].reshape(-1, *a.shape)
        gathered.append(joined_along(tiles, dim))
        at += a.size
    return tuple(gathered)


def in_blocks(value, dim, length):
    before, after = (value.shape[:dim], value.shape[dim + 1 :])
    return jnp.moveaxis(value.reshape(*before, length, -1, *after), dim, 0)


def sum_at_owner(value, axis, dim):
    tiles = in_blocks(value, dim, lax.axis_size(axis))
    arrived = lax.all_to_all(tiles, axis, split_axis=0, concat_axis=0, tiled=True)
    return arrived.astype(jnp.float32).sum(axis=0)


def copy_for_each(value, axis):
    length = lax.axis_size(axis)
    return lax.all_to_all(
        jnp.broadcast_to(value[None], (length, *value.shape)), axis, 0, 0, tiled=True
    )


def taken_together(value, axis):
    everything = copy_for_each(value, axis)
    return jnp.sum(everything.astype(jnp.float32), axis=0)


def dequantize(codes, scale_codes, col_scale):
    block_count = codes.shape[0]
    columns = codes.shape[2]
    nibbles = jnp.stack([codes >> 4 * nibble_pos & 15 for nibble_pos in range(4)], axis=2)
    levels = jnp.zeros(nibbles.shape, jnp.float32)
    for position, quantum in enumerate(nf4_table):
        levels = jnp.where(nibbles == position, jnp.float32(quantum), levels)
    absmax = (scale_codes.astype(jnp.float32) + 1.0) / 256.0 * col_scale[None, :]
    weight = levels * absmax[:, None, None, :]
    return weight.reshape(block_count * 64, columns).astype(jnp.bfloat16)


def local(acts, grad_out, codes, scale_codes, col_scale, down_adapter, up_adapter):
    down_full, up_full = gather_packed((down_adapter, up_adapter), "fsdp", (1, 1))
    mixed = jnp.dot(grad_out, up_full.T, preferred_element_type=jnp.float32).astype(jnp.bfloat16)
    lowered = jnp.dot(acts, down_full.T, preferred_element_type=jnp.float32).astype(jnp.bfloat16)
    token_count = acts.shape[0] * lax.axis_size("dp") * lax.axis_size("fsdp")
    scale_factor = adapter_scale * float(token_count) ** (-0.5)
    local_rows = dequantize(codes, scale_codes, col_scale)
    frozen_base = lax.dot_general(
        grad_out,
        lax.all_gather(local_rows, "fsdp", axis=0, tiled=True),
        (((1,), (1,)), ((), ())),
        preferred_element_type=jnp.float32,
    )
    operand_side = jnp.dot(mixed, down_full, preferred_element_type=jnp.float32)
    input_gradient = (frozen_base + adapter_scale * operand_side).astype(jnp.bfloat16)
    term_down = lax.dot_general(
        mixed, acts, (((0,), (0,)), ((), ())), preferred_element_type=jnp.float32
    )
    term_up = lax.dot_general(
        lowered, grad_out, (((0,), (0,)), ((), ())), preferred_element_type=jnp.float32
    )
    shard_down = sum_at_owner(term_down.astype(jnp.bfloat16), "fsdp", 1)
    shard_up = sum_at_owner(term_up.astype(jnp.bfloat16), "fsdp", 1)
    summed_down = taken_together(shard_down.astype(jnp.bfloat16), "dp").astype(jnp.float32)
    summed_up = taken_together(shard_up.astype(jnp.bfloat16), "dp").astype(jnp.float32)
    grad_down = scale_factor * summed_down
    grad_up = scale_factor * summed_up
    return (input_gradient, grad_down, grad_up)


def solution(mesh):
    placed = (
        P(("dp", "fsdp"), None),
        P(("dp", "fsdp"), None),
        P("fsdp", None, None),
        P("fsdp", None),
        P(),
        P(None, "fsdp"),
        P(None, "fsdp"),
    )
    return jax.shard_map(
        local,
        mesh=mesh,
        in_specs=placed,
        out_specs=(P(("dp", "fsdp"), None), P(None, "fsdp"), P(None, "fsdp")),
        check_vma=False,
    )
```

profile of v0, /device:TPU:1, one launch (start us, length us, event | category | flops | bytes accessed | tf_op | source)
XLA Modules:
  0.0 462.1 jit_solution(7870341430328449806)
XLA Ops:
  7.2 1.0 copy.31
  8.2 1.4 pad_maximum_fusion
  9.7 1.5 and_bitcast_fusion.3
  11.2 0.9 copy-done.2
  12.5 4.1 select_select_fusion
  16.6 4.8 %copy.23 = f32[16,16,4,1024]{3,2,1,0:T(4,128)} copy(f32[16,16,4,1024]{3,1,0,2:T(8,128)S(1)} %select_select_fusion) | data formatting | bytes 8388608 | tf_op jit(solution)/shard_map/jit(_where)/select_n | solution.py:72
  21.5 5.3 %reshape.108 = f32[1024,1024]{1,0:T(8,128)} reshape(f32[16,16,4,1024]{3,2,1,0:T(4,128)} %copy.23) | data formatting | bytes 8388608 | tf_op jit(solution)/shard_map/jit(_where)/select_n | solution.py:72
  26.8 2.2 fusion.1
  29.0 2.1 copy.22
  31.8 3.1 mul.45
  34.9 5.3 %mul.46 = f32[1024,1024]{1,0:T(8,128)} reshape(f32[16,16,4,1024]{3,2,1,0:T(4,128)} %mul.45) | data formatting | bytes 8388608 | tf_op jit(solution)/shard_map/mul | solution.py:74
  40.2 6.0 %multiply_convert_fusion = bf16[1024,1024]{1,0:T(8,128)(2,1)} fusion(f32[1024,1024]{1,0:T(8,128)} %mul.46, pred[1024,1024]{1,0:T(8,128)(4,1)S(1)} %eq.156, f32[1024,1024]{1,0:T(8,128)} %reshape.108), kind=kLoop, calls=%fused_computation.6 | loop fusion | flops 3145728 | bytes 11534336 | tf_op jit(solution)/shard_map/convert_element_type | solution.py:75
  46.3 2.7 all-gather.6.cloned.1.call-done
  49.0 1.8 reshape.92
  51.4 6.3 %fusion.2 = bf16[8,8,8,128]{3,2,1,0:T(8,128)(2,1)S(1)} fusion(bf16[512,1024]{1,0:T(8,128)(2,1)S(1)} %copy-done, bf16[64,8192]{1,0:T(8,128)(2,1)S(1)} %bitcast.52, bf16[512,8192]{1,0:T(8,128)(2,1)} %param.7), kind=kOutput, calls=%fused_computation.9 | convolution fusion | flops 604078080 | bytes 10616832 | tf_op jit(solution)/shard_map/dot_general | solution.py:96
  58.4 4.1 all-to-all-start.2
  63.0 5.6 %convolution_convert_fusion = bf16[64,8192]{1,0:T(8,128)(2,1)S(1)} fusion(bf16[64,512]{1,0:T(8,128)(2,1)S(1)} %convolution_convert_fusion.2, bf16[512,8192]{1,0:T(8,128)(2,1)} %param.7), kind=kOutput, calls=%fused_computation.2 | convolution fusion | flops 537395200 | bytes 9502720 | tf_op jit(solution)/shard_map/dot_general | solution.py:93
  68.6 1.1 copy.40
  69.7 5.1 %all-to-all-start = ((bf16[8,64,1024]{2,1,0:T(8,128)(2,1)}), bf16[8,64,1024]{2,1,0:T(8,128)(2,1)S(1)}, u32[]{:S(2)}, u32[]{:S(2)}) async-start(bf16[8,64,1024]{2,1,0:T(8,128)(2,1)} %bitcast.54), calls=%async_computation | async-start | bytes 2097152 | tf_op jit(solution)/shard_map/all_to_all | solution.py:50
  74.8 25.6 %all-to-all-done = bf16[8,64,1024]{2,1,0:T(8,128)(2,1)S(1)} async-done(((bf16[8,64,1024]{2,1,0:T(8,128)(2,1)}), bf16[8,64,1024]{2,1,0:T(8,128)(2,1)S(1)}, u32[]{:S(2)}, u32[]{:S(2)}) %all-to-all-start) | async-done | bytes 1048608 | tf_op jit(solution)/shard_map/all_to_all | solution.py:50
  100.3 0.8 broadcast_in_dim.84
  101.1 12.4 %all-to-all-start.3 = ((bf16[16,64,128]{2,1,0:T(8,128)(2,1)}), bf16[16,64,128]{2,1,0:T(8,128)(2,1)S(1)}, u32[]{:S(2)}, u32[]{:S(2)}) async-start(bf16[16,64,128]{2,1,0:T(8,128)(2,1)} %broadcast_in_dim.84), calls=%async_computation.3 | async-start | bytes 524288 | tf_op jit(solution)/shard_map/all_to_all | solution.py:56
  113.5 0.8 reduce_sum.42
  114.4 11.2 %all-to-all-done.3 = bf16[16,64,128]{2,1,0:T(8,128)(2,1)S(1)} async-done(((bf16[16,64,128]{2,1,0:T(8,128)(2,1)}), bf16[16,64,128]{2,1,0:T(8,128)(2,1)S(1)}, u32[]{:S(2)}, u32[]{:S(2)}) %all-to-all-start.3) | async-done | bytes 262176 | tf_op jit(solution)/shard_map/all_to_all | solution.py:56
  125.5 2.5 broadcast_in_dim.83
  128.0 5.0 %all-to-all-start.1 = ((bf16[16,64,1024]{2,1,0:T(8,128)(2,1)}), bf16[16,64,1024]{2,1,0:T(8,128)(2,1)}, u32[]{:S(2)}, u32[]{:S(2)}) async-start(bf16[16,64,1024]{2,1,0:T(8,128)(2,1)} %broadcast_in_dim.83), calls=%async_computation.1 | async-start | bytes 4194304 | tf_op jit(solution)/shard_map/all_to_all | solution.py:56
  133.7 50.9 %all-to-all-done.1 = bf16[16,64,1024]{2,1,0:T(8,128)(2,1)} async-done(((bf16[16,64,1024]{2,1,0:T(8,128)(2,1)}), bf16[16,64,1024]{2,1,0:T(8,128)(2,1)}, u32[]{:S(2)}, u32[]{:S(2)}) %all-to-all-start.1) | async-done | bytes 2097184 | tf_op jit(solution)/shard_map/all_to_all | solution.py:56
  184.6 2.0 convert_reduce_fusion
  187.3 230.9 %all-gather.4.cloned.1.call-done = bf16[8192,1024]{1,0:T(8,128)(2,1)} async-done(((bf16[1024,1024]{1,0:T(8,128)(2,1)}), bf16[8192,1024]{1,0:T(8,128)(2,1)}) %all-gather.4.cloned.1.call-update) | async-done | bytes 16777232 | tf_op jit(solution)/shard_map/all_gather | solution.py:87
  418.3 15.8 %fusion.5 = f32[8192,512]{1,0:T(8,128)} fusion(bf16[8192,1024]{1,0:T(8,128)(2,1)} %all-gather.4.cloned.1.call-done, bf16[512,1024]{1,0:T(8,128)(2,1)S(1)} %copy-done), kind=kOutput, calls=%fused_computation.26 | convolution fusion | flops 8589934592 | bytes 34603008 | tf_op jit(solution)/shard_map/dot_general | solution.py:85
  434.0 9.2 %fusion = bf16[512,8192]{0,1:T(8,128)(2,1)} fusion(f32[8192,512]{1,0:T(8,128)} %fusion.5, bf16[64,512]{1,0:T(8,128)(2,1)S(1)} %convolution_convert_fusion.2, bf16[64,8192]{1,0:T(8,128)(2,1)S(1)} %bitcast.53), kind=kOutput, calls=%fused_computation.1 | convolution fusion | flops 549453824 | bytes 26279936 | tf_op jit(solution)/shard_map/dot_general | solution.py:91
  443.3 12.0 %copy.27 = bf16[512,8192]{1,0:T(8,128)(2,1)} copy(bf16[512,8192]{0,1:T(8,128)(2,1)} %fusion) | data formatting | bytes 16777216
  (28 shorter events, 4.4 us)
Async XLA Ops:
  7.2 44.3 %copy-start = (bf16[512,1024]{1,0:T(8,128)(2,1)S(1)}, bf16[512,1024]{1,0:T(8,128)(2,1)}, u32[]{:S(2)}) copy-start(bf16[512,1024]{1,0:T(8,128)(2,1)} %param.8) | copy-start | bytes 3145732
  7.2 41.8 %all-gather.6.cloned.1.call-start = ((), (), s32[]{:S(2)}) async-start(), calls=%async_computation.5 | async-start | bytes 1327104 | tf_op jit(solution)/shard_map/all_gather | solution.py:35
  9.6 408.6 %all-gather.4.cloned.1.call-start = ((), (), s32[]{:S(2)}) async-start(), calls=%async_computation.4 | async-start | bytes 18874368 | tf_op jit(solution)/shard_map/all_gather | solution.py:87
  11.2 1.0 copy-start.2
  11.2 1.3 copy-start.3
  26.8 5.0 %copy-start.5 = (f32[1024]{0:T(1024)S(1)}, f32[1024]{0:T(1024)}, u32[]{:S(2)}) copy-start(f32[1024]{0:T(1024)} %param.11) | copy-start | bytes 12292
  26.8 5.0 %copy-start.4 = (s32[16,1024]{1,0:T(8,128)S(1)}, s32[16,1024]{1,0:T(8,128)}, u32[]{:S(2)}) copy-start(s32[16,1024]{1,0:T(8,128)} %param.10) | copy-start | bytes 196612
  58.4 11.2 %all-to-all-start.2 = ((bf16[8,64,128]{2,1,0:T(8,128)(2,1)}), bf16[8,64,128]{2,1,0:T(8,128)(2,1)S(1)}, u32[]{:S(2)}, u32[]{:S(2)}) async-start(bf16[8,64,128]{2,1,0:T(8,128)(2,1)} %bitcast.51), calls=%async_computation.2 | async-start | bytes 262144 | tf_op jit(solution)/shard_map/all_to_all | solution.py:50
  69.7 30.7 %all-to-all-start = ((bf16[8,64,1024]{2,1,0:T(8,128)(2,1)}), bf16[8,64,1024]{2,1,0:T(8,128)(2,1)S(1)}, u32[]{:S(2)}, u32[]{:S(2)}) async-start(bf16[8,64,1024]{2,1,0:T(8,128)(2,1)} %bitcast.54), calls=%async_computation | async-start | bytes 2097152 | tf_op jit(solution)/shard_map/all_to_all | solution.py:50
  101.1 24.4 %all-to-all-start.3 = ((bf16[16,64,128]{2,1,0:T(8,128)(2,1)}), bf16[16,64,128]{2,1,0:T(8,128)(2,1)S(1)}, u32[]{:S(2)}, u32[]{:S(2)}) async-start(bf16[16,64,128]{2,1,0:T(8,128)(2,1)} %broadcast_in_dim.84), calls=%async_computation.3 | async-start | bytes 524288 | tf_op jit(solution)/shard_map/all_to_all | solution.py:56
  128.0 56.5 %all-to-all-start.1 = ((bf16[16,64,1024]{2,1,0:T(8,128)(2,1)}), bf16[16,64,1024]{2,1,0:T(8,128)(2,1)}, u32[]{:S(2)}, u32[]{:S(2)}) async-start(bf16[16,64,1024]{2,1,0:T(8,128)(2,1)} %broadcast_in_dim.83), calls=%async_computation.1 | async-start | bytes 4194304 | tf_op jit(solution)/shard_map/all_to_all | solution.py:56
  443.3 12.0 %copy-start.1 = (bf16[512,1024]{1,0:T(8,128)(2,1)S(1)}, bf16[512,1024]{1,0:T(8,128)(2,1)}, u32[]{:S(2)}) copy-start(bf16[512,1024]{1,0:T(8,128)(2,1)} %param.8) | copy-start | bytes 3145732
Sparse Core Ops, SparseCore 0:
  10.2 38.7 all-gather.5
  51.2 367.0 all-gather.3
where the time goes:
time: 463 us; the launch traced here: 462 us
  waiting for transfers between devices  321 us (69%)
  local copies, waits for them, and re-layouts  43.1 us (9%)
  matrix products  37.4 us (8%)
  starting transfers between devices  26.7 us (6%)
  other arithmetic  19.5 us (4%)
  between operations  14.2 us (3%)
    all_gather x1, waiting for transfers between devices, local(): lax.all_gather(local_rows, 'fsdp', axis=0, tiled=True)  231 us
    all_to_all x2, waiting for transfers between devices, copy_for_each(): lax.all_to_all(jnp.broadcast_to(value[None], (length, *value.shape)), axi...  62 us
    all_to_all x2, waiting for transfers between devices, sum_at_owner(): lax.all_to_all(tiles, axis, split_axis=0, concat_axis=0, tiled=True)  25.6 us
    all_to_all x2, starting transfers between devices, copy_for_each(): lax.all_to_all(jnp.broadcast_to(value[None], (length, *value.shape)), axi...  17.4 us
    dot_general x1, matrix products, local(): lax.dot_general(grad_out, lax.all_gather(local_rows, 'fsdp', axis=0, tile...  15.8 us
    unnamed x15, local copies, waits for them, and re-layouts  14.9 us
    select_n x2, local copies, waits for them, and re-layouts, dequantize(): levels = jnp.where(nibbles == position, jnp.float32(quantum), levels)  10.2 us
  transfers between devices with their start and end apart: 6, of which 5 were waited for; matrix products, arithmetic and copies ran while one was open for 13% of the time, Pallas kernels for 0%

commit v1 on v0

--- a/solution.py
+++ b/solution.py
@@ -1,3 +1,4 @@
+import functools
 import jax
 import jax.numpy as jnp
 from jax import lax
@@ -22,6 +23,16 @@
     0.7229568362236023,
     1.0,
 ]
+
+
+def rails_end(arr, dim_no):
+    local_out = lax.axis_size("fsdp")
+    inter = jnp.stack([arr] * local_out)
+    part_next = lax.all_to_all(inter, "fsdp", split_axis=0, concat_axis=0)
+    return jnp.concatenate(part_next, axis=dim_no)
+
+
+track_frame = functools.partial(rails_end, dim_no=0)
 
 
 def joined_along(tiles, dim):
@@ -84,7 +95,7 @@
     local_rows = dequantize(codes, scale_codes, col_scale)
     frozen_base = lax.dot_general(
         grad_out,
-        lax.all_gather(local_rows, "fsdp", axis=0, tiled=True),
+        track_frame(local_rows),
         (((1,), (1,)), ((), ())),
         preferred_element_type=jnp.float32,
     )

time: 463 us -> 391 us (0.84)
  waiting for transfers between devices: 321 us -> 233 us
  starting transfers between devices: 26.7 us -> 33.4 us
  local copies, waits for them, and re-layouts: 43.1 us -> 49.2 us
    all_gather x1 -> x0, waiting for transfers between devices: 231 us -> none  [local(): lax.all_gather(local_rows, 'fsdp', axis=0, tiled=True)]
    all_to_all x0 -> x1, waiting for transfers between devices: none -> 180 us  [rails_end(): part_next = lax.all_to_all(inter, 'fsdp', split_axis=0, concat_axis=0)]
    all_to_all x2, waiting for transfers between devices: 62 us -> 3.51 us  [copy_for_each(): lax.all_to_all(jnp.broadcast_to(value[None], (length, *value.shape)), axi...]
    all_gather x1, waiting for transfers between devices: 2.66 us -> 39.3 us  [gather_packed(): lines, at, gathered = (lax.all_gather(flat, axis), 0, [])]
    all_to_all x2, waiting for transfers between devices: 25.6 us -> 10.4 us  [sum_at_owner(): lax.all_to_all(tiles, axis, split_axis=0, concat_axis=0, tiled=True)]
    another operation x0 -> x1, local copies, waits for them, and re-layouts: none -> 6.02 us  [rails_end(): inter = jnp.stack([arr] * local_out)]
    all_to_all x0 -> x1, starting transfers between devices: none -> 5.97 us  [rails_end(): part_next = lax.all_to_all(inter, 'fsdp', split_axis=0, concat_axis=0)]
  transfers between devices with their start and end apart: 6 -> 6, of which waited for: 5 -> 4; matrix products, arithmetic and copies ran while one was open for 13% -> 13% of each run, Pallas kernels for 0% -> 0%
where the time goes in v1:
time: 391 us; the launch traced here: 389 us
  waiting for transfers between devices  233 us (60%)
  local copies, waits for them, and re-layouts  49.2 us (13%)
  matrix products  36.7 us (9%)
  starting transfers between devices  33.4 us (9%)
  other arithmetic  22.4 us (6%)
  between operations  14.2 us (4%)
    all_to_all x1, waiting for transfers between devices, rails_end(): part_next = lax.all_to_all(inter, 'fsdp', split_axis=0, concat_axis=0)  180 us
    all_gather x1, waiting for transfers between devices, gather_packed(): lines, at, gathered = (lax.all_gather(flat, axis), 0, [])  39.3 us
    all_to_all x2, starting transfers between devices, copy_for_each(): lax.all_to_all(jnp.broadcast_to(value[None], (length, *value.shape)), axi...  19 us
    dot_general x1, matrix products, local(): lax.dot_general(grad_out, track_frame(local_rows), (((1,), (1,)), ((), ()...  15.8 us
    unnamed x15, local copies, waits for them, and re-layouts  13.8 us
    all_to_all x2, waiting for transfers between devices, sum_at_owner(): lax.all_to_all(tiles, axis, split_axis=0, concat_axis=0, tiled=True)  10.4 us
    select_n x2, local copies, waits for them, and re-layouts, dequantize(): levels = jnp.where(nibbles == position, jnp.float32(quantum), levels)  10.1 us
    dot_general x1, matrix products, local(): operand_side = jnp.dot(mixed, down_full, preferred_element_type=jnp.float32)  9.21 us
  transfers between devices with their start and end apart: 6, of which 4 were waited for; matrix products, arithmetic and copies ran while one was open for 13% of the time, Pallas kernels for 0%

profile of v1, /device:TPU:1, one launch (start us, length us, event | category | flops | bytes accessed | tf_op | source)
XLA Modules:
  0.0 389.4 jit_solution(3053156096834672124)
XLA Ops:
  7.2 1.0 copy.31
  8.2 1.4 pad_maximum_fusion
  9.6 39.3 %all-gather.3.cloned.1.call-done = bf16[589824]{0:T(1024)(128)(2,1)} async-done(((bf16[73728]{0:T(1024)(128)(2,1)}), bf16[589824]{0:T(1024)(128)(2,1)}) %all-gather.3.cloned.1.call-update) | async-done | bytes 1179664 | tf_op jit(solution)/shard_map/all_gather | solution.py:46
  49.0 1.8 reshape.101
  51.9 6.3 %fusion.2 = bf16[8,8,8,128]{3,2,1,0:T(8,128)(2,1)S(1)} fusion(bf16[512,1024]{1,0:T(8,128)(2,1)S(1)} %copy-done, bf16[64,8192]{1,0:T(8,128)(2,1)S(1)} %bitcast.53, bf16[512,8192]{1,0:T(8,128)(2,1)} %param.7), kind=kOutput, calls=%fused_computation.9 | convolution fusion | flops 604078080 | bytes 10616832 | tf_op jit(solution)/shard_map/dot_general | solution.py:107
  58.9 3.4 all-to-all-start.3
  62.3 5.0 %convolution_convert_fusion = bf16[64,8192]{1,0:T(8,128)(2,1)S(1)} fusion(bf16[64,512]{1,0:T(8,128)(2,1)S(1)} %convolution_convert_fusion.2, bf16[512,8192]{1,0:T(8,128)(2,1)} %param.7), kind=kOutput, calls=%fused_computation.2 | convolution fusion | flops 537395200 | bytes 9502720 | tf_op jit(solution)/shard_map/dot_general | solution.py:104
  67.2 1.1 copy.40
  68.3 5.1 %all-to-all-start.1 = ((bf16[8,64,1024]{2,1,0:T(8,128)(2,1)}), bf16[8,64,1024]{2,1,0:T(8,128)(2,1)S(1)}, u32[]{:S(2)}, u32[]{:S(2)}) async-start(bf16[8,64,1024]{2,1,0:T(8,128)(2,1)} %bitcast.50), calls=%async_computation.1 | async-start | bytes 2097152 | tf_op jit(solution)/shard_map/all_to_all | solution.py:61
  73.4 10.4 %all-to-all-done.1 = bf16[8,64,1024]{2,1,0:T(8,128)(2,1)S(1)} async-done(((bf16[8,64,1024]{2,1,0:T(8,128)(2,1)}), bf16[8,64,1024]{2,1,0:T(8,128)(2,1)S(1)}, u32[]{:S(2)}, u32[]{:S(2)}) %all-to-all-start.1) | async-done | bytes 1048608 | tf_op jit(solution)/shard_map/all_to_all | solution.py:61
  84.8 13.9 %all-to-all-start.4 = ((bf16[16,64,128]{2,1,0:T(8,128)(2,1)}), bf16[16,64,128]{2,1,0:T(8,128)(2,1)S(1)}, u32[]{:S(2)}, u32[]{:S(2)}) async-start(bf16[16,64,128]{2,1,0:T(8,128)(2,1)} %broadcast_in_dim.84), calls=%async_computation.4 | async-start | bytes 524288 | tf_op jit(solution)/shard_map/all_to_all | solution.py:67
  98.7 3.1 and_bitcast_fusion.3
  101.8 2.1 reduce_sum.42
  103.9 3.5 all-to-all-done.4
  107.4 2.5 broadcast_in_dim.83
  109.9 5.1 %all-to-all-start.2 = ((bf16[16,64,1024]{2,1,0:T(8,128)(2,1)}), bf16[16,64,1024]{2,1,0:T(8,128)(2,1)}, u32[]{:S(2)}, u32[]{:S(2)}) async-start(bf16[16,64,1024]{2,1,0:T(8,128)(2,1)} %broadcast_in_dim.83), calls=%async_computation.2 | async-start | bytes 4194304 | tf_op jit(solution)/shard_map/all_to_all | solution.py:67
  115.0 5.2 %select_select_fusion = f32[16,16,4,1024]{3,1,0,2:T(8,128)S(1)} fusion(s32[16,16,1,1024]{3,1,0,2:T(8,128)} %get-tuple-element.17, s32[16,16,1,1024]{3,1,0,2:T(8,128)} %get-tuple-element.18, s32[16,16,1,1024]{3,1,0,2:T(8,128)S(1)} %get-tuple-element.16, s32[16,16,1,1024]{3,1,0,2:T(8,128)S(1)} %get-tuple-element.15), kind=kLoop, calls=%fused_computation.4 | loop fusion | flops 34603008 | bytes 8388608 | tf_op jit(solution)/shard_map/jit(_where)/select_n | solution.py:83
  120.2 4.8 %copy.23 = f32[16,16,4,1024]{3,2,1,0:T(4,128)} copy(f32[16,16,4,1024]{3,1,0,2:T(8,128)S(1)} %select_select_fusion) | data formatting | bytes 8388608 | tf_op jit(solution)/shard_map/jit(_where)/select_n | solution.py:83
  125.0 5.3 %reshape.117 = f32[1024,1024]{1,0:T(8,128)} reshape(f32[16,16,4,1024]{3,2,1,0:T(4,128)} %copy.23) | data formatting | bytes 8388608 | tf_op jit(solution)/shard_map/jit(_where)/select_n | solution.py:83
  130.3 2.2 fusion.1
  132.5 2.1 copy.22
  134.6 1.9 eq.188
  136.5 3.1 mul.47
  139.6 5.3 %mul.48 = f32[1024,1024]{1,0:T(8,128)} reshape(f32[16,16,4,1024]{3,2,1,0:T(4,128)} %mul.47) | data formatting | bytes 8388608 | tf_op jit(solution)/shard_map/mul | solution.py:85
  144.9 5.0 %multiply_convert_fusion = bf16[1024,1024]{1,0:T(8,128)(2,1)S(1)} fusion(f32[1024,1024]{1,0:T(8,128)} %mul.48, pred[1024,1024]{1,0:T(8,128)(4,1)} %eq.188, f32[1024,1024]{1,0:T(8,128)} %reshape.117), kind=kLoop, calls=%fused_computation.6 | loop fusion | flops 3145728 | bytes 11534336 | tf_op jit(solution)/shard_map/convert_element_type | solution.py:86
  149.9 6.0 %stack.31 = bf16[8,1024,1024]{2,1,0:T(8,128)(2,1)} broadcast(bf16[1024,1024]{1,0:T(8,128)(2,1)S(1)} %multiply_convert_fusion), dimensions={1,2} | broadcast | bytes 18874368 | tf_op jit(solution)/shard_map/stack | solution.py:30
  155.9 6.0 %all-to-all-start = ((bf16[8,1024,1024]{2,1,0:T(8,128)(2,1)}), bf16[8,1024,1024]{2,1,0:T(8,128)(2,1)}, u32[]{:S(2)}, u32[]{:S(2)}) async-start(bf16[8,1024,1024]{2,1,0:T(8,128)(2,1)} %stack.31), calls=%async_computation | async-start | bytes 33554432 | tf_op jit(solution)/shard_map/all_to_all | solution.py:31
  162.6 2.0 convert_reduce_fusion
  165.3 180.3 %all-to-all-done = bf16[8,1024,1024]{2,1,0:T(8,128)(2,1)} async-done(((bf16[8,1024,1024]{2,1,0:T(8,128)(2,1)}), bf16[8,1024,1024]{2,1,0:T(8,128)(2,1)}, u32[]{:S(2)}, u32[]{:S(2)}) %all-to-all-start) | async-done | bytes 16777248 | tf_op jit(solution)/shard_map/all_to_all | solution.py:31
  345.6 15.8 %fusion.5 = f32[8192,512]{1,0:T(8,128)} fusion(bf16[8192,1024]{1,0:T(8,128)(2,1)} %bitcast.4, bf16[512,1024]{1,0:T(8,128)(2,1)S(1)} %copy-done), kind=kOutput, calls=%fused_computation.26 | convolution fusion | flops 8589934592 | bytes 34603008 | tf_op jit(solution)/shard_map/dot_general | solution.py:96
  361.5 9.2 %fusion = bf16[512,8192]{0,1:T(8,128)(2,1)} fusion(f32[8192,512]{1,0:T(8,128)} %fusion.5, bf16[64,512]{1,0:T(8,128)(2,1)S(1)} %convolution_convert_fusion.2, bf16[64,8192]{1,0:T(8,128)(2,1)S(1)} %bitcast.54), kind=kOutput, calls=%fused_computation.1 | convolution fusion | flops 549453824 | bytes 26279936 | tf_op jit(solution)/shard_map/dot_general | solution.py:102
  370.7 11.9 %copy.27 = bf16[512,8192]{1,0:T(8,128)(2,1)} copy(bf16[512,8192]{0,1:T(8,128)(2,1)} %fusion) | data formatting | bytes 16777216
  (28 shorter events, 4.4 us)
Async XLA Ops:
  7.2 44.3 %copy-start = (bf16[512,1024]{1,0:T(8,128)(2,1)S(1)}, bf16[512,1024]{1,0:T(8,128)(2,1)}, u32[]{:S(2)}) copy-start(bf16[512,1024]{1,0:T(8,128)(2,1)} %param.8) | copy-start | bytes 3145732
  7.2 41.8 %all-gather.3.cloned.1.call-start = ((), (), s32[]{:S(2)}) async-start(), calls=%async_computation.5 | async-start | bytes 1327104 | tf_op jit(solution)/shard_map/all_gather | solution.py:46
  51.4 6.8 %copy-start.1 = (bf16[8,8,8,1024]{3,1,2,0:T(8,128)(2,1)}, bf16[8,8,8,1024]{3,1,2,0:T(8,128)(2,1)S(1)}, u32[]{:S(2)}) copy-start(bf16[8,8,8,1024]{3,1,2,0:T(8,128)(2,1)S(1)} %copy.33) | copy-start | bytes 3145732
  58.9 9.4 %all-to-all-start.3 = ((bf16[8,64,128]{2,1,0:T(8,128)(2,1)}), bf16[8,64,128]{2,1,0:T(8,128)(2,1)S(1)}, u32[]{:S(2)}, u32[]{:S(2)}) async-start(bf16[8,64,128]{2,1,0:T(8,128)(2,1)} %bitcast.52), calls=%async_computation.3 | async-start | bytes 262144 | tf_op jit(solution)/shard_map/all_to_all | solution.py:61
  68.3 15.5 %all-to-all-start.1 = ((bf16[8,64,1024]{2,1,0:T(8,128)(2,1)}), bf16[8,64,1024]{2,1,0:T(8,128)(2,1)S(1)}, u32[]{:S(2)}, u32[]{:S(2)}) async-start(bf16[8,64,1024]{2,1,0:T(8,128)(2,1)} %bitcast.50), calls=%async_computation.1 | async-start | bytes 2097152 | tf_op jit(solution)/shard_map/all_to_all | solution.py:61
  83.7 1.1 copy-start.3
  84.8 22.6 %all-to-all-start.4 = ((bf16[16,64,128]{2,1,0:T(8,128)(2,1)}), bf16[16,64,128]{2,1,0:T(8,128)(2,1)S(1)}, u32[]{:S(2)}, u32[]{:S(2)}) async-start(bf16[16,64,128]{2,1,0:T(8,128)(2,1)} %broadcast_in_dim.84), calls=%async_computation.4 | async-start | bytes 524288 | tf_op jit(solution)/shard_map/all_to_all | solution.py:67
  109.9 40.0 %all-to-all-start.2 = ((bf16[16,64,1024]{2,1,0:T(8,128)(2,1)}), bf16[16,64,1024]{2,1,0:T(8,128)(2,1)}, u32[]{:S(2)}, u32[]{:S(2)}) async-start(bf16[16,64,1024]{2,1,0:T(8,128)(2,1)} %broadcast_in_dim.83), calls=%async_computation.2 | async-start | bytes 4194304 | tf_op jit(solution)/shard_map/all_to_all | solution.py:67
  130.3 6.2 %copy-start.5 = (f32[1024]{0:T(1024)S(1)}, f32[1024]{0:T(1024)}, u32[]{:S(2)}) copy-start(f32[1024]{0:T(1024)} %param.11) | copy-start | bytes 12292
  130.3 6.2 %copy-start.4 = (s32[16,1024]{1,0:T(8,128)S(1)}, s32[16,1024]{1,0:T(8,128)}, u32[]{:S(2)}) copy-start(s32[16,1024]{1,0:T(8,128)} %param.10) | copy-start | bytes 196612
  155.9 189.7 %all-to-all-start = ((bf16[8,1024,1024]{2,1,0:T(8,128)(2,1)}), bf16[8,1024,1024]{2,1,0:T(8,128)(2,1)}, u32[]{:S(2)}, u32[]{:S(2)}) async-start(bf16[8,1024,1024]{2,1,0:T(8,128)(2,1)} %stack.31), calls=%async_computation | async-start | bytes 33554432 | tf_op jit(solution)/shard_map/all_to_all | solution.py:31
  345.6 15.9 %copy-start.2 = (bf16[8,8,8,1024]{3,1,2,0:T(8,128)(2,1)S(1)}, bf16[8,8,8,1024]{3,1,2,0:T(8,128)(2,1)}, u32[]{:S(2)}) copy-start(bf16[8,8,8,1024]{3,1,2,0:T(8,128)(2,1)} %copy-done.1) | copy-start | bytes 3145732
Sparse Core Ops, SparseCore 0:
  10.2 38.7 all-gather.2
